TPU v7x, 32 devices: a whole 2x2x4 slice. The times are simulated.
32 devices in a mesh: shard: 4 (over z), replica: 8 (over y, x, core).
Axes of the slice: x: 2, y: 2, z: 4, core: 2. Of those that a mesh axis runs over, the one named last changes fastest.
Arguments:
- atom_feats: bfloat16 [2048, 9, 128], P(('shard', 'replica')), may hold values from -6 to 6
- cotangent: bfloat16 [2048, 9, 128], P(('shard', 'replica')), may hold values from -6 to 6
- frames: bfloat16 [9, 9, 8192], P(None, None, ('shard', 'replica')), may hold values from -2 to 2
- radial: bfloat16 [8192, 128], P(('shard', 'replica')), may hold values from 0.19921875 to 2
- edge_source: int32 [8192], P(('shard', 'replica')), may hold values from 0 to 63
- edge_target: int32 [8192], P(('shard', 'replica')), may hold values from 0 to 63
- edge_valid: int32 [8192], P(('shard', 'replica')), may hold values 0 or 1
- atom_types: int32 [2048], P(('shard', 'replica')), may hold values from 0 to 99
- dataset: int32 [32], P(('shard', 'replica')), may hold values from 0 to 4
- type_table: float32 [100, 128], replicated, may hold values from -6 to 6
- dataset_table: float32 [5, 128], replicated, may hold values from -6 to 6
- router_weight: float32 [128, 28], replicated, may hold values from -1.5 to 1.5
- experts: bfloat16 [28, 384, 384], P(None, 'shard'), may hold values from -3 to 3
Outputs:
- updated: bfloat16 [2048, 9, 128], P(('shard', 'replica'))
- feats_grad: float32 [2048, 9, 128], P(('shard', 'replica'))
- expert_grad: float32 [28, 384, 384], P(None, 'shard')
Inputs may be any that keep to these rules, and one draw needn't show every extreme that they name: `edge_source`: indices of atoms within the edge's own system. `edge_target`: indices of atoms within the edge's own system.
All inputs are finite; a program needn't handle non-finite values. No bound on the sum of `edge_valid` on one device may be relied on, other than what follows from the above.
Results may differ from a plain program's by a relative error of at most 0.011.
Values may be sent and summed in bfloat16 or wider, within the bound.
A program may use at most 64 MiB of HBM per device.

v0:
```python
import math
import jax
import jax.numpy as jnp
from jax import lax
from jax.sharding import PartitionSpec as P


def system_mix(type_rows, dataset_one, type_table, dataset_table, router_weight):
    table_size = type_table.shape[0]
    onehot = (type_rows[:, None] == jnp.arange(table_size, dtype=jnp.int32)[None, :]).astype(
        jnp.float32
    )
    counts = jnp.sum(onehot, axis=0)
    embed = jnp.dot(counts, type_table, precision=lax.Precision.HIGHEST) / type_rows.shape[0]
    pick = (
        dataset_one[:, None] == jnp.arange(dataset_table.shape[0], dtype=jnp.int32)[None, :]
    ).astype(jnp.float32)
    embed = embed + jnp.dot(pick, dataset_table, precision=lax.Precision.HIGHEST)[0]
    soft = jax.nn.softplus(jnp.dot(embed, router_weight, precision=lax.Precision.HIGHEST))
    return soft / jnp.sum(soft)


def edge_layer(feats32, merged32, frames, radial, source, target, valid):
    atom_count, components, channels = feats32.shape
    edge_count = source.shape[0]
    top_degree = math.isqrt(components) - 1
    feats = feats32.astype(jnp.bfloat16)
    merged = merged32.astype(jnp.bfloat16)
    gathered = jnp.take(feats, source, axis=0)
    rotated = jnp.einsum(
        "ije,ejc->eic", frames.astype(jnp.float32), gathered.astype(jnp.float32)
    ).astype(jnp.bfloat16)
    zero_rows = [degree * degree + degree for degree in range(top_degree + 1)]
    zero_band = jnp.concatenate(
        [rotated[:, row : row + 1, :] for row in zero_rows], axis=1
    ).reshape(edge_count, -1)
    mixed_band = jnp.dot(zero_band, merged, preferred_element_type=jnp.float32).reshape(
        edge_count, top_degree + 1, channels
    )
    columns = []
    for column in range(components):
        if column in zero_rows:
            columns.append(mixed_band[:, zero_rows.index(column), :])
        else:
            columns.append(rotated[:, column, :].astype(jnp.float32))
    combined = jnp.stack(columns, axis=1)
    message = (combined * radial.astype(jnp.float32)[:, None, :]).astype(jnp.bfloat16)
    unrotated = jnp.einsum(
        "jie,ejc->eic", frames.astype(jnp.float32), message.astype(jnp.float32)
    ).astype(jnp.bfloat16)
    incidence = (
        (target[None, :] == jnp.arange(atom_count, dtype=jnp.int32)[:, None]) & (valid[None, :] > 0)
    ).astype(jnp.bfloat16)
    summed = jnp.dot(
        incidence, unrotated.reshape(edge_count, -1), preferred_element_type=jnp.float32
    )
    return feats32 + summed.reshape(atom_count, components, channels) * (atom_count / edge_count)


def add_system(total, pair):
    mix_row, rows = pair
    term = lax.optimization_barrier((mix_row[:, None, None] * rows[None]).astype(jnp.bfloat16))
    return (total + term.astype(jnp.float32), None)


def shards(
    atom_feats,
    cotangent,
    frames,
    radial,
    edge_source,
    edge_target,
    edge_valid,
    atom_types,
    dataset,
    type_table,
    dataset_table,
    router_weight,
    experts,
):
    group = lax.axis_size("shard")
    row_block = experts.shape[1]
    row_total = row_block * group
    mixture = system_mix(atom_types, dataset, type_table, dataset_table, router_weight)
    group_mixtures = lax.all_gather(mixture[None, :], "shard", axis=0, tiled=True)
    row_shares = jnp.einsum(
        "sk,krc->src", group_mixtures, experts.astype(jnp.float32), precision=lax.Precision.HIGHEST
    ).astype(jnp.bfloat16)
    merged = lax.all_to_all(row_shares, "shard", split_axis=0, concat_axis=1, tiled=True).reshape(
        row_total, -1
    )
    merged32 = lax.optimization_barrier(merged).astype(jnp.float32)

    def local(feats32, weight32):
        return edge_layer(feats32, weight32, frames, radial, edge_source, edge_target, edge_valid)

    result, pullback = jax.vjp(local, atom_feats.astype(jnp.float32), merged32)
    feats_grad, weight_grad = pullback(cotangent.astype(jnp.float32))
    back_mixtures = lax.all_gather(mixture[None, :], "shard", axis=0, tiled=True)
    received = lax.all_to_all(
        weight_grad.reshape(group, row_block, -1).astype(jnp.bfloat16),
        "shard",
        split_axis=0,
        concat_axis=0,
        tiled=True,
    ).astype(jnp.float32)
    start = jnp.zeros(experts.shape, jnp.float32)
    shard_sum, unused = lax.scan(add_system, start, (back_mixtures, received))
    expert_grad = lax.psum(shard_sum, "replica")
    return (result.astype(jnp.bfloat16), feats_grad, expert_grad)


def solution(mesh):
    in_specs = (
        P(("shard", "replica"), None, None),
        P(("shard", "replica"), None, None),
        P(None, None, ("shard", "replica")),
        P(("shard", "replica"), None),
        P(("shard", "replica")),
        P(("shard", "replica")),
        P(("shard", "replica")),
        P(("shard", "replica")),
        P(("shard", "replica")),
        P(),
        P(),
        P(),
        P(None, "shard", None),
    )
    out_specs = (
        P(("shard", "replica"), None, None),
        P(("shard", "replica"), None, None),
        P(None, "shard", None),
    )
    return jax.shard_map(shards, mesh=mesh, in_specs=in_specs, out_specs=out_specs, check_vma=False)
```

profile of v0, /device:TPU:0, one launch (start us, length us, event | category | flops | bytes accessed | tf_op | source)
XLA Modules:
  0.0 189.4 jit_solution(16895955329291108513)
XLA Ops:
  8.0 0.7 convert_reduce_fusion
  8.8 1.2 dynamic-slice
  10.7 0.8 convolution_bitcast_fusion.1
  11.5 1.0 fusion.12
  12.5 1.5 fusion.55
  14.0 0.7 divide_dynamic-update-slice_fusion
  14.7 13.5 %all-reduce.11 = f32[112]{0:T(128)S(1)} all-reduce(f32[112]{0:T(128)S(1)} %divide_dynamic-update-slice_fusion), channel_id=2, replica_groups=mesh['shard'=4,'replica'=8] {'shard'}, use_global_device_ids=true, to_apply=%add.11 | all-reduce | flops 112 | bytes 896
  28.2 1.4 fusion.5
  29.6 0.7 copy.100
  30.4 3.5 %all-to-all-start = ((bf16[4,96,384]{2,1,0:T(8,128)(2,1)}), bf16[4,96,384]{2,1,0:T(8,128)(2,1)S(1)}, u32[]{:S(2)}, u32[]{:S(2)}) async-start(bf16[4,96,384]{2,1,0:T(8,128)(2,1)} %copy.100), calls=%async_computation | async-start | bytes 589824 | tf_op jit(solution)/shard_map/all_to_all | solution.py:89
  33.8 0.5 compare_and_fusion
  34.4 0.6 pad_clamp_fusion
  35.0 0.7 convert_element_type.132
  35.7 1.2 convolution_convert_fusion
  36.8 1.3 copy.109
  38.2 1.7 copy.110
  39.9 1.9 copy.97
  41.8 3.8 %gather_fusion = bf16[256,9,128]{2,0,1:T(8,128)(2,1)} fusion(bf16[64,9,128]{2,0,1:T(8,128)(2,1)S(1)} %copy-done.1, s32[1024]{0:T(1024)} %pad_clamp_fusion), kind=kCustom, calls=%fused_computation | custom fusion | bytes 1180672 | tf_op jit(solution)/shard_map/jvp(jit(_take))/gather | solution.py:29
  45.5 1.2 broadcast_select_fusion
  46.7 0.5 fusion.2
  47.3 1.6 slice_convert_fusion
  48.9 1.2 pad_maximum_fusion
  50.0 1.8 copy.98
  51.8 2.6 %fusion.56 = (bf16[256,9,128]{2,1,0:T(8,128)(2,1)}, f32[256,9,128]{2,1,0:T(8,128)S(1)}) fusion(f32[256,128]{1,0:T(8,128)} %convert_element_type.132, bf16[256,9,128]{2,1,0:T(8,128)(2,1)} %copy.110, bf16[9,9,256]{1,0,2:T(8,128)(2,1)S(1)} %copy.97), kind=kOutput, calls=%fused_computation.91 | convolution fusion | flops 6488064 | bytes 2531840 | tf_op jit(solution)/shard_map/transpose(jvp(jie,ejc->eic))/dot_general | solution.py:48
  54.5 0.2 fusion.51
  54.7 0.4 fusion.33
  55.1 0.2 copy.112
  55.4 1.0 fusion.58
  56.4 5.0 %all-to-all-start.1 = ((bf16[4,96,384]{2,1,0:T(8,128)(2,1)}), bf16[4,96,384]{2,1,0:T(8,128)(2,1)}, u32[]{:S(2)}, u32[]{:S(2)}) async-start(bf16[4,96,384]{2,1,0:T(8,128)(2,1)} %bitcast.24), calls=%async_computation.1 | async-start | bytes 589824 | tf_op jit(solution)/shard_map/all_to_all | solution.py:100
  61.5 0.7 reshape.81
  62.1 1.9 %copy.106 = bf16[9,9,256]{0,1,2:T(8,128)(2,1)S(1)} copy(bf16[9,9,256]{2,1,0:T(8,128)(2,1)} %param.17) | data formatting | bytes 82944 | tf_op args[2]
  64.0 4.0 %fusion.52 = (bf16[256,1,128]{2,1,0:T(2,128)(2,1)}, bf16[256,1,128]{2,1,0:T(2,128)(2,1)}, bf16[256,1,128]{2,1,0:T(2,128)(2,1)}, bf16[256,1,128]{2,1,0:T(2,128)(2...) fusion(bf16[256,9,128]{2,1,0:T(8,128)(2,1)} %get-tuple-element.74), kind=kLoop, calls=%fused_computation.87 | loop fusion | bytes 786432 | tf_op jit(solution)/shard_map/transpose(jvp())/unstack | solution.py:46
  68.1 0.9 copy.101
  69.0 1.8 convert_element_type.147
  70.8 25.5 %while.11 = (s32[]{:T(128)}, f32[28,96,384]{2,1,0:T(8,128)}, f32[4,28]{1,0:T(4,128)}, f32[4,96,384]{2,1,0:T(8,128)}, s32[]{:T(128)}, /*index=5*/s32[]{:T(128)}) while((s32[]{:T(128)}, f32[28,96,384]{2,1,0:T(8,128)}, f32[4,28]{1,0:T(4,128)}, f32[4,96,384]{2,1,0:T(8,128)}, s32[]{:T(128)}, /*index=5*/s32[]{:T(128)}) %tuple.48), condition=%wide.region_4.5_spmd.clone, body=%wide.region_3.4_spmd.clone.sunk | while | flops 5160963 | bytes 12829103 | solution.py:108
  70.8 0.7 dynamic-slice_bitcast_fusion.5
  71.4 0.9 dynamic-slice_bitcast_fusion.4
  72.4 0.5 multiply_convert_fusion.4
  72.9 2.7 %select_add_fusion.2 = f32[28,96,384]{2,1,0:T(8,128)} fusion(f32[28,96,384]{2,1,0:T(8,128)} %get-tuple-element.108, bf16[28,96,384]{2,1,0:T(8,128)(2,1)S(1)} %multiply_convert_fusion.4, pred[]{:T(512)S(6)} %compare.14), kind=kLoop, calls=%fused_computation.2.clone.1 | loop fusion | flops 3096576 | bytes 10321921 | tf_op jit(solution)/shard_map/while/body/eval_jaxpr/add | solution.py:63
  75.5 0.7 dynamic-slice_bitcast_fusion.5
  76.2 0.9 dynamic-slice_bitcast_fusion.4
  77.1 0.5 multiply_convert_fusion.4
  77.6 4.8 %select_add_fusion.2 = f32[28,96,384]{2,1,0:T(8,128)} fusion(f32[28,96,384]{2,1,0:T(8,128)} %get-tuple-element.108, bf16[28,96,384]{2,1,0:T(8,128)(2,1)S(1)} %multiply_convert_fusion.4, pred[]{:T(512)S(6)} %compare.14), kind=kLoop, calls=%fused_computation.2.clone.1 | loop fusion | flops 3096576 | bytes 10321921 | tf_op jit(solution)/shard_map/while/body/eval_jaxpr/add | solution.py:63
  82.4 0.7 dynamic-slice_bitcast_fusion.5
  83.1 0.9 dynamic-slice_bitcast_fusion.4
  84.0 0.5 multiply_convert_fusion.4
  84.5 4.8 %select_add_fusion.2 = f32[28,96,384]{2,1,0:T(8,128)} fusion(f32[28,96,384]{2,1,0:T(8,128)} %get-tuple-element.108, bf16[28,96,384]{2,1,0:T(8,128)(2,1)S(1)} %multiply_convert_fusion.4, pred[]{:T(512)S(6)} %compare.14), kind=kLoop, calls=%fused_computation.2.clone.1 | loop fusion | flops 3096576 | bytes 10321921 | tf_op jit(solution)/shard_map/while/body/eval_jaxpr/add | solution.py:63
  89.4 0.7 dynamic-slice_bitcast_fusion.5
  90.0 0.9 dynamic-slice_bitcast_fusion.4
  91.0 0.5 multiply_convert_fusion.4
  91.4 4.8 %select_add_fusion.2 = f32[28,96,384]{2,1,0:T(8,128)} fusion(f32[28,96,384]{2,1,0:T(8,128)} %get-tuple-element.108, bf16[28,96,384]{2,1,0:T(8,128)(2,1)S(1)} %multiply_convert_fusion.4, pred[]{:T(512)S(6)} %compare.14), kind=kLoop, calls=%fused_computation.2.clone.1 | loop fusion | flops 3096576 | bytes 10321921 | tf_op jit(solution)/shard_map/while/body/eval_jaxpr/add | solution.py:63
  96.3 1.4 fusion.57
  97.7 0.8 fusion.53
  98.4 7.0 %stack.2 = f32[256,9,128]{2,1,0:T(8,128)} concatenate(f32[256,1,128]{2,1,0:T(1,128)} %bitcast.98, f32[256,1,128]{2,1,0:T(1,128)} %get-tuple-element.62, f32[256,1,128]{2,1,0:T(1,128)} %bitcast.97, f32[256,1,128]{2,1,0:T(1,128)} %get-tuple-element.61, f32[256,1,128]{2,1,0:T(1,128)} %get-tuple-element.60, f32[256,1,128]{2,1,0:T(1,128)} %get-tuple-element.59, ...), dimensions={1} | concatenate | bytes 2359296 | tf_op jit(solution)/shard_map/jvp()/stack | solution.py:46
  105.4 3.0 %fusion.3 = bf16[256,9,128]{2,1,0:T(8,128)(2,1)} fusion(bf16[9,9,256]{0,1,2:T(8,128)(2,1)S(1)} %copy.106, f32[256,9,128]{2,1,0:T(8,128)} %stack.2, f32[256,128]{1,0:T(8,128)} %convert_element_type.132), kind=kOutput, calls=%fused_computation.16 | convolution fusion | flops 6193152 | bytes 1942016 | tf_op jit(solution)/shard_map/jvp(jie,ejc->eic)/dot_general | solution.py:48
  108.5 2.4 %copy.107 = bf16[256,9,128]{0,2,1:T(8,128)(2,1)} copy(bf16[256,9,128]{2,1,0:T(8,128)(2,1)} %fusion.3) | data formatting | bytes 1179648 | tf_op jit(solution)/shard_map/jvp()/convert_element_type | solution.py:50
  110.8 1.2 fusion.59
  112.5 0.8 copy.126
  113.3 3.9 %fusion.4 = bf16[256,9,128]{2,1,0:T(8,128)(2,1)S(1)} fusion(bf16[9,9,256]{0,1,2:T(8,128)(2,1)} %copy-done.2, bf16[256,1,128]{2,1,0:T(2,128)(2,1)} %copy.126, bf16[256,1,128]{2,1,0:T(2,128)(2,1)S(1)} %copy.125, bf16[256,1,128]{2,1,0:T(2,128)(2,1)S(1)} %copy.124, bf16[256,1,128]{2,1,0:T(2,128)(2,1)} %get-tuple-element.52, ...), kind=kOutput, calls=%fused_computation.17 | convolution fusion | flops 10911744 | bytes 1221120 | tf_op jit(solution)/shard_map/transpose(jvp(ije,ejc->eic))/dot_general | solution.py:30
  117.3 9.3 %scatter_fusion = bf16[64,9,128]{2,1,0:T(8,128)(2,1)S(1)} fusion(bf16[64,9,128]{2,1,0:T(8,128)(2,1)S(1)} %broadcast_in_dim.24, s32[256]{0:T(256)S(1)} %copy-done.8, bf16[256,9,128]{2,1,0:T(8,128)(2,1)S(1)} %fusion.4), kind=kCustom, calls=%fused_computation.1 | custom fusion | flops 294912 | bytes 1770496 | tf_op jit(solution)/shard_map/transpose(jvp(jit(_take)))/scatter-add | solution.py:29
  126.6 1.7 convert_add_fusion
  128.3 2.1 %fusion.9 = bf16[64,9,128]{2,0,1:T(8,128)(2,1)} fusion(bf16[256,9,128]{0,2,1:T(8,128)(2,1)} %copy.107, bf16[64,9,128]{2,0,1:T(8,128)(2,1)S(1)} %copy-done.1, s32[256]{0:T(256)S(1)} %copy-done.10, pred[256]{0:T(512)(128)(4,1)S(1)} %copy-done.12), kind=kOutput, calls=%fused_computation.23 | convolution fusion | flops 38076416 | bytes 886016 | tf_op jit(solution)/shard_map/jvp()/dot_general | solution.py:54
  130.4 47.8 %all-reduce.14.cloned.1.call-done = f32[28,96,384]{2,1,0:T(8,128)} async-done(((f32[28,96,384]{2,1,0:T(8,128)}), f32[28,96,384]{2,1,0:T(8,128)}) %all-reduce.14.cloned.1.call-update) | async-done | bytes 4128784 | tf_op jit(solution)/shard_map/psum | solution.py:109
  178.2 4.4 %copy.149 = f32[28,96,384]{2,1,0:T(8,128)} copy(f32[28,96,384]{2,1,0:T(8,128)} %all-reduce.14.cloned.1.call-done) | data formatting | bytes 8257536
  (50 shorter events, 0.8 us)
Async XLA Ops:
  7.2 21.1 %copy-start = (bf16[28,96,384]{2,1,0:T(8,128)(2,1)S(1)}, bf16[28,96,384]{2,1,0:T(8,128)(2,1)}, u32[]{:S(2)}) copy-start(bf16[28,96,384]{2,1,0:T(8,128)(2,1)} %param.27) | copy-start | bytes 6193156
  7.2 26.7 %copy-start.15 = (s32[256]{0:T(256)S(1)}, s32[256]{0:T(256)}, u32[]{:S(2)}) copy-start(s32[256]{0:T(256)} %param.19) | copy-start | bytes 3076
  7.2 27.1 %copy-start.17 = (s32[256]{0:T(256)S(1)}, s32[256]{0:T(256)}, u32[]{:S(2)}) copy-start(s32[256]{0:T(256)} %param.21) | copy-start | bytes 3076
  7.2 27.8 %copy-start.6 = (bf16[256,128]{1,0:T(8,128)(2,1)S(1)}, bf16[256,128]{1,0:T(8,128)(2,1)}, u32[]{:S(2)}) copy-start(bf16[256,128]{1,0:T(8,128)(2,1)} %param.18) | copy-start | bytes 196612
  7.2 28.4 %copy-start.9 = (s32[256]{0:T(256)S(1)}, s32[256]{0:T(256)}, u32[]{:S(2)}) copy-start(s32[256]{0:T(256)} %param.20) | copy-start | bytes 3076
  7.2 28.4 %copy-start.5 = (bf16[64,9,128]{2,0,1:T(8,128)(2,1)S(1)}, bf16[64,9,128]{2,0,1:T(8,128)(2,1)}, u32[]{:S(2)}) copy-start(bf16[64,9,128]{2,0,1:T(8,128)(2,1)} %param.16) | copy-start | bytes 442372
  28.2 6.2 %copy-start.13 = (f32[112]{0:T(128)}, f32[112]{0:T(128)S(1)}, u32[]{:S(2)}) copy-start(f32[112]{0:T(128)S(1)} %all-reduce.11) | copy-start | bytes 1348
  30.4 26.0 %all-to-all-start = ((bf16[4,96,384]{2,1,0:T(8,128)(2,1)}), bf16[4,96,384]{2,1,0:T(8,128)(2,1)S(1)}, u32[]{:S(2)}, u32[]{:S(2)}) async-start(bf16[4,96,384]{2,1,0:T(8,128)(2,1)} %copy.100), calls=%async_computation | async-start | bytes 589824 | tf_op jit(solution)/shard_map/all_to_all | solution.py:89
  34.3 1.3 copy-start.7
  34.4 1.3 copy-start.11
  36.8 4.9 %copy-start.1 = (bf16[64,9,128]{2,0,1:T(8,128)(2,1)S(1)}, bf16[64,9,128]{2,0,1:T(8,128)(2,1)}, u32[]{:S(2)}) copy-start(bf16[64,9,128]{2,0,1:T(8,128)(2,1)} %param.15) | copy-start | bytes 442372
  51.8 2.9 %copy-start.16 = (pred[3]{0:T(512)(128)(4,1)S(1)}, pred[3]{0:T(512)(128)(4,1)}, u32[]{:S(2)}) copy-start(pred[3]{0:T(512)(128)(4,1)} %constant.42.clone.1) | copy-start | bytes 13
  54.5 0.9 copy-start.3
  54.5 7.0 %copy-start.14 = (f32[112]{0:T(128)S(1)}, f32[112]{0:T(128)}, u32[]{:S(2)}) copy-start(f32[112]{0:T(128)} %copy-done.13) | copy-start | bytes 1348
  55.2 6.2 %copy-start.4 = (bf16[256,3,128]{0,2,1:T(8,128)(2,1)}, bf16[256,3,128]{0,2,1:T(8,128)(2,1)S(1)}, u32[]{:S(2)}) copy-start(bf16[256,3,128]{0,2,1:T(8,128)(2,1)S(1)} %copy.112) | copy-start | bytes 589828
  56.4 12.6 %all-to-all-start.1 = ((bf16[4,96,384]{2,1,0:T(8,128)(2,1)}), bf16[4,96,384]{2,1,0:T(8,128)(2,1)}, u32[]{:S(2)}, u32[]{:S(2)}) async-start(bf16[4,96,384]{2,1,0:T(8,128)(2,1)} %bitcast.24), calls=%async_computation.1 | async-start | bytes 589824 | tf_op jit(solution)/shard_map/all_to_all | solution.py:100
  61.4 116.7 %all-reduce.14.cloned.1.call-start = ((), (), s32[]{:S(2)}) async-start(), calls=%async_computation.2 | async-start | bytes 8257536 | tf_op jit(solution)/shard_map/psum | solution.py:109
  64.0 41.4 %copy-start.2 = (bf16[9,9,256]{0,1,2:T(8,128)(2,1)}, bf16[9,9,256]{0,1,2:T(8,128)(2,1)S(1)}, u32[]{:S(2)}) copy-start(bf16[9,9,256]{0,1,2:T(8,128)(2,1)S(1)} %copy.106) | copy-start | bytes 124420
  113.3 4.0 %copy-start.8 = (s32[256]{0:T(256)S(1)}, s32[256]{0:T(256)}, u32[]{:S(2)}) copy-start(s32[256]{0:T(256)} %copy-done.7) | copy-start | bytes 3076
  117.3 11.0 %copy-start.10 = (s32[256]{0:T(256)S(1)}, s32[256]{0:T(256)}, u32[]{:S(2)}) copy-start(s32[256]{0:T(256)} %param.20) | copy-start | bytes 3076
  117.3 11.0 %copy-start.12 = (pred[256]{0:T(512)(128)(4,1)S(1)}, pred[256]{0:T(512)(128)(4,1)}, u32[]{:S(2)}) copy-start(pred[256]{0:T(512)(128)(4,1)} %copy-done.11) | copy-start | bytes 772
Sparse Core Ops, SparseCore 0:
  96.4 81.6 all-reduce.13
where the time goes:
time: 191 us; the launch traced here: 189 us
  waiting for transfers between devices  47.8 us (25%)
  local copies, waits for them, and re-layouts  42.7 us (22%)
  other arithmetic  39.5 us (21%)
  matrix products  21.6 us (11%)
  between operations  15.8 us (8%)
  blocking collectives  13.5 us (7%)
  starting transfers between devices  8.5 us (4%)
    psum x1, waiting for transfers between devices, shards(): expert_grad = lax.psum(shard_sum, 'replica')  47.8 us
    add x4, other arithmetic, add_system(): return (total + term.astype(jnp.float32), None)  17.2 us
    unnamed x1, blocking collectives  13.5 us
    another operation x3, local copies, waits for them, and re-layouts, edge_layer(): combined = jnp.stack(columns, axis=1)  11.2 us
    unnamed x44, local copies, waits for them, and re-layouts  10.7 us
    scatter-add x1, other arithmetic, edge_layer(): gathered = jnp.take(feats, source, axis=0)  9.32 us
    mul x8, local copies, waits for them, and re-layouts, add_system(): mix_row[:, None, None] * rows[None]  6.35 us
    dot_general x2, matrix products, edge_layer(): jnp.einsum('jie,ejc->eic', frames.astype(jnp.float32), message.astype(jnp...  5.67 us
  transfers between devices with their start and end apart: 3, of which 1 were waited for; matrix products, arithmetic and copies ran while one was open for 34% of the time, Pallas kernels for 0%

commit v1 on v0

--- a/solution.py
+++ b/solution.py
@@ -3,6 +3,16 @@
 import jax.numpy as jnp
 from jax import lax
 from jax.sharding import PartitionSpec as P
+
+
+def post_spans(block_here):
+    n_peers_all = jax.lax.axis_size("replica")
+    work_now = block_here
+    for tick in [q for q in (1, 2, 4, 8, 16) if q < n_peers_all]:
+        work_now = work_now + jax.lax.ppermute(
+            work_now, "replica", [(at, at ^ tick) for at in range(n_peers_all)]
+        )
+    return work_now
 
 
 def system_mix(type_rows, dataset_one, type_table, dataset_table, router_weight):
@@ -106,7 +116,7 @@
     ).astype(jnp.float32)
     start = jnp.zeros(experts.shape, jnp.float32)
     shard_sum, unused = lax.scan(add_system, start, (back_mixtures, received))
-    expert_grad = lax.psum(shard_sum, "replica")
+    expert_grad = post_spans(shard_sum)
     return (result.astype(jnp.bfloat16), feats_grad, expert_grad)
 
 

time: 191 us -> 266 us (1.39)
  waiting for transfers between devices: 47.8 us -> 140 us
  local copies, waits for them, and re-layouts: 42.7 us -> 27.7 us
  between operations: 15.8 us -> 2.24 us
  other arithmetic: 39.5 us -> 50.1 us
  starting transfers between devices: 8.5 us -> 12.9 us
    ppermute x0 -> x3, waiting for transfers between devices: none -> 137 us  [post_spans(): jax.lax.ppermute(work_now, 'replica', [(at, at ^ tick) for at in range(n_...]
    psum x1 -> x0, waiting for transfers between devices: 47.8 us -> none  [shards(): expert_grad = lax.psum(shard_sum, 'replica')]
    add x0 -> x3, other arithmetic: none -> 11.1 us  [post_spans(): work_now + jax.lax.ppermute(work_now, 'replica', [(at, at ^ tick) for at...]
    mul x8, local copies, waits for them, and re-layouts: 6.35 us -> 0.07 us  [add_system(): mix_row[:, None, None] * rows[None]]
    unnamed x44 -> x41, local copies, waits for them, and re-layouts: 10.7 us -> 4.6 us
    all_to_all x1, waiting for transfers between devices: 0.01 us -> 3.14 us  [shards(): lax.all_to_all(row_shares, 'shard', split_axis=0, concat_axis=1, tiled=True)]
    ppermute x0 -> x3, starting transfers between devices: none -> 3.08 us  [post_spans(): jax.lax.ppermute(work_now, 'replica', [(at, at ^ tick) for at in range(n_...]
  transfers between devices with their start and end apart: 3 -> 5, of which waited for: 1 -> 4; matrix products, arithmetic and copies ran while one was open for 34% -> 17% of each run, Pallas kernels for 0% -> 0%
where the time goes in v1:
time: 266 us; the launch traced here: 265 us
  waiting for transfers between devices  140 us (53%)
  other arithmetic  50.1 us (19%)
  local copies, waits for them, and re-layouts  27.7 us (10%)
  matrix products  19.6 us (7%)
  starting transfers between devices  12.9 us (5%)
  blocking collectives  12.3 us (5%)
    ppermute x3, waiting for transfers between devices, post_spans(): jax.lax.ppermute(work_now, 'replica', [(at, at ^ tick) for at in range(n_...  137 us
    add x4, other arithmetic, add_system(): return (total + term.astype(jnp.float32), None)  17.2 us
    unnamed x1, blocking collectives  12.3 us
    another operation x3, local copies, waits for them, and re-layouts, edge_layer(): combined = jnp.stack(columns, axis=1)  11.1 us
    add x3, other arithmetic, post_spans(): work_now + jax.lax.ppermute(work_now, 'replica', [(at, at ^ tick) for at...  11.1 us
    scatter-add x1, other arithmetic, edge_layer(): gathered = jnp.take(feats, source, axis=0)  9.32 us
    all_to_all x1, starting transfers between devices, shards(): lax.all_to_all(weight_grad.reshape(group, row_block, -1).astype(jnp.bfloa...  6.35 us
    dot_general x2, matrix products, edge_layer(): jnp.einsum('jie,ejc->eic', frames.astype(jnp.float32), message.astype(jnp...  5.77 us
  transfers between devices with their start and end apart: 5, of which 4 were waited for; matrix products, arithmetic and copies ran while one was open for 17% of the time, Pallas kernels for 0%

profile of v1, /device:TPU:0, one launch (start us, length us, event | category | flops | bytes accessed | tf_op | source)
XLA Modules:
  0.0 264.7 jit_solution(13097486189877065902)
XLA Ops:
  0.7 0.9 compare_and_fusion
  1.5 0.7 compare_select_fusion
  2.2 0.7 broadcast_compare_fusion
  2.9 1.5 convert_element_type.132
  4.4 1.3 convolution_convert_fusion
  5.7 0.2 copy.109
  6.0 1.7 copy.110
  7.7 1.0 copy.97
  8.7 3.6 %gather_fusion = bf16[256,9,128]{2,0,1:T(8,128)(2,1)} fusion(bf16[64,9,128]{2,0,1:T(8,128)(2,1)S(1)} %copy-done.1, s32[1024]{0:T(1024)S(1)} %pad_clamp_fusion), kind=kCustom, calls=%fused_computation | custom fusion | bytes 1180672 | tf_op jit(solution)/shard_map/jvp(jit(_take))/gather | solution.py:39
  12.3 1.2 broadcast_select_fusion
  13.5 0.5 fusion.2
  14.0 1.6 slice_convert_fusion
  15.6 1.2 pad_maximum_fusion
  16.8 1.1 copy.98
  17.9 2.7 %fusion.56 = (bf16[256,9,128]{2,1,0:T(8,128)(2,1)}, f32[256,9,128]{2,1,0:T(8,128)S(1)}) fusion(f32[256,128]{1,0:T(8,128)} %convert_element_type.132, bf16[256,9,128]{2,1,0:T(8,128)(2,1)} %copy.110, bf16[9,9,256]{1,0,2:T(8,128)(2,1)S(1)} %copy.97), kind=kOutput, calls=%fused_computation.91 | convolution fusion | flops 6488064 | bytes 2531840 | tf_op jit(solution)/shard_map/transpose(jvp(jie,ejc->eic))/dot_general | solution.py:58
  20.7 0.2 fusion.51
  20.9 0.4 fusion.33
  21.3 0.2 copy.112
  21.5 1.0 fusion.58
  22.5 6.3 %all-to-all-start.1 = ((bf16[4,96,384]{2,1,0:T(8,128)(2,1)}), bf16[4,96,384]{2,1,0:T(8,128)(2,1)S(1)}, u32[]{:S(2)}, u32[]{:S(2)}) async-start(bf16[4,96,384]{2,1,0:T(8,128)(2,1)} %bitcast.24), calls=%async_computation.1 | async-start | bytes 589824 | tf_op jit(solution)/shard_map/all_to_all | solution.py:110
  29.6 0.6 dynamic-slice
  30.8 0.1 convolution_bitcast_fusion.1
  30.9 0.2 fusion.12
  31.1 0.8 fusion.55
  31.9 0.7 divide_dynamic-update-slice_fusion
  32.7 12.3 %all-reduce.11 = f32[112]{0:T(128)S(1)} all-reduce(f32[112]{0:T(128)S(1)} %divide_dynamic-update-slice_fusion), channel_id=2, replica_groups=mesh['shard'=4,'replica'=8] {'shard'}, use_global_device_ids=true, to_apply=%add.11 | all-reduce | flops 112 | bytes 896
  45.1 19.3 %while.11 = (s32[]{:T(128)}, f32[28,96,384]{2,1,0:T(8,128)}, f32[4,28]{1,0:T(4,128)S(1)}, f32[4,96,384]{2,1,0:T(8,128)S(1)}, s32[]{:T(128)}, /*index=5*/s32[]{:T(128)}) while((s32[]{:T(128)}, f32[28,96,384]{2,1,0:T(8,128)}, f32[4,28]{1,0:T(4,128)S(1)}, f32[4,96,384]{2,1,0:T(8,128)S(1)}, s32[]{:T(128)}, /*index=5*/s32[]{:T(128)}) %tuple.48), condition=%wide.region_4.5_spmd.clone, body=%wide.region_3.4_spmd.clone.sunk | while | flops 5160963 | bytes 12829103 | solution.py:118
  45.2 0.5 multiply_convert_fusion.4
  45.7 2.7 %select_add_fusion.2 = f32[28,96,384]{2,1,0:T(8,128)} fusion(f32[28,96,384]{2,1,0:T(8,128)} %get-tuple-element.108, bf16[28,96,384]{2,1,0:T(8,128)(2,1)S(1)} %multiply_convert_fusion.4, pred[]{:T(512)S(6)} %compare.14), kind=kLoop, calls=%fused_computation.2.clone.1 | loop fusion | flops 3096576 | bytes 10321921 | tf_op jit(solution)/shard_map/while/body/eval_jaxpr/add | solution.py:73
  48.4 0.5 multiply_convert_fusion.4
  48.9 4.8 %select_add_fusion.2 = f32[28,96,384]{2,1,0:T(8,128)} fusion(f32[28,96,384]{2,1,0:T(8,128)} %get-tuple-element.108, bf16[28,96,384]{2,1,0:T(8,128)(2,1)S(1)} %multiply_convert_fusion.4, pred[]{:T(512)S(6)} %compare.14), kind=kLoop, calls=%fused_computation.2.clone.1 | loop fusion | flops 3096576 | bytes 10321921 | tf_op jit(solution)/shard_map/while/body/eval_jaxpr/add | solution.py:73
  53.7 0.5 multiply_convert_fusion.4
  54.2 4.8 %select_add_fusion.2 = f32[28,96,384]{2,1,0:T(8,128)} fusion(f32[28,96,384]{2,1,0:T(8,128)} %get-tuple-element.108, bf16[28,96,384]{2,1,0:T(8,128)(2,1)S(1)} %multiply_convert_fusion.4, pred[]{:T(512)S(6)} %compare.14), kind=kLoop, calls=%fused_computation.2.clone.1 | loop fusion | flops 3096576 | bytes 10321921 | tf_op jit(solution)/shard_map/while/body/eval_jaxpr/add | solution.py:73
  59.1 0.5 multiply_convert_fusion.4
  59.5 4.8 %select_add_fusion.2 = f32[28,96,384]{2,1,0:T(8,128)} fusion(f32[28,96,384]{2,1,0:T(8,128)} %get-tuple-element.108, bf16[28,96,384]{2,1,0:T(8,128)(2,1)S(1)} %multiply_convert_fusion.4, pred[]{:T(512)S(6)} %compare.14), kind=kLoop, calls=%fused_computation.2.clone.1 | loop fusion | flops 3096576 | bytes 10321921 | tf_op jit(solution)/shard_map/while/body/eval_jaxpr/add | solution.py:73
  64.4 7.3 %collective-permute-done = f32[28,96,384]{2,1,0:T(8,128)S(1)} collective-permute-done((f32[28,96,384]{2,1,0:T(8,128)}, f32[28,96,384]{2,1,0:T(8,128)S(1)}, u32[]{:S(2)}, u32[]{:S(2)}) %collective-permute-start) | collective-permute-done | bytes 4128800 | tf_op jit(solution)/shard_map/ppermute | solution.py:12
  71.7 2.7 %add.62 = f32[28,96,384]{2,1,0:T(8,128)S(1)} add(f32[28,96,384]{2,1,0:T(8,128)} %get-tuple-element.25, f32[28,96,384]{2,1,0:T(8,128)S(1)} %collective-permute-done) | non-fusion elementwise | flops 1032192 | bytes 12386304 | tf_op jit(solution)/shard_map/add | solution.py:12
  74.4 1.6 collective-permute-start.1
  76.0 89.7 %collective-permute-done.1 = f32[28,96,384]{2,1,0:T(8,128)S(1)} collective-permute-done((f32[28,96,384]{2,1,0:T(8,128)S(1)}, f32[28,96,384]{2,1,0:T(8,128)S(1)}, u32[]{:S(2)}, u32[]{:S(2)}) %collective-permute-start.1) | collective-permute-done | bytes 4128800 | tf_op jit(solution)/shard_map/ppermute | solution.py:12
  165.7 2.4 add.63
  168.1 1.5 collective-permute-start.2
  169.7 1.4 fusion.5
  171.1 0.7 copy.100
  171.9 3.5 %all-to-all-start = ((bf16[4,96,384]{2,1,0:T(8,128)(2,1)}), bf16[4,96,384]{2,1,0:T(8,128)(2,1)S(1)}, u32[]{:S(2)}, u32[]{:S(2)}) async-start(bf16[4,96,384]{2,1,0:T(8,128)(2,1)} %copy.100), calls=%async_computation | async-start | bytes 589824 | tf_op jit(solution)/shard_map/all_to_all | solution.py:99
  175.3 1.9 copy.106
  177.2 3.9 %fusion.52 = (bf16[256,1,128]{2,1,0:T(2,128)(2,1)}, bf16[256,1,128]{2,1,0:T(2,128)(2,1)}, bf16[256,1,128]{2,1,0:T(2,128)(2,1)}, bf16[256,1,128]{2,1,0:T(2,128)(2...) fusion(bf16[256,9,128]{2,1,0:T(8,128)(2,1)} %get-tuple-element.74), kind=kLoop, calls=%fused_computation.87 | loop fusion | bytes 786432 | tf_op jit(solution)/shard_map/transpose(jvp())/unstack | solution.py:56
  181.2 3.1 %all-to-all-done = bf16[4,96,384]{2,1,0:T(8,128)(2,1)S(1)} async-done(((bf16[4,96,384]{2,1,0:T(8,128)(2,1)}), bf16[4,96,384]{2,1,0:T(8,128)(2,1)S(1)}, u32[]{:S(2)}, u32[]{:S(2)}) %all-to-all-start) | async-done | bytes 294944 | tf_op jit(solution)/shard_map/all_to_all | solution.py:99
  184.3 0.9 copy.101
  185.2 1.4 fusion.57
  186.6 0.8 fusion.53
  187.4 6.9 %stack.2 = f32[256,9,128]{2,1,0:T(8,128)} concatenate(f32[256,1,128]{2,1,0:T(1,128)} %bitcast.98, f32[256,1,128]{2,1,0:T(1,128)} %get-tuple-element.62, f32[256,1,128]{2,1,0:T(1,128)} %bitcast.97, f32[256,1,128]{2,1,0:T(1,128)} %get-tuple-element.61, f32[256,1,128]{2,1,0:T(1,128)} %get-tuple-element.60, f32[256,1,128]{2,1,0:T(1,128)} %get-tuple-element.59, ...), dimensions={1} | concatenate | bytes 2359296 | tf_op jit(solution)/shard_map/jvp()/stack | solution.py:56
  194.3 3.1 %fusion.3 = bf16[256,9,128]{2,1,0:T(8,128)(2,1)} fusion(bf16[9,9,256]{0,1,2:T(8,128)(2,1)S(1)} %copy.106, f32[256,9,128]{2,1,0:T(8,128)} %stack.2, f32[256,128]{1,0:T(8,128)} %convert_element_type.132), kind=kOutput, calls=%fused_computation.16 | convolution fusion | flops 6193152 | bytes 1942016 | tf_op jit(solution)/shard_map/jvp(jie,ejc->eic)/dot_general | solution.py:58
  197.4 2.4 copy.107
  199.7 1.2 fusion.59
  201.0 0.1 copy.113
  201.1 0.1 copy.124
  201.3 0.1 copy.125
  201.4 0.8 copy.126
  202.2 3.9 %fusion.4 = bf16[256,9,128]{2,1,0:T(8,128)(2,1)S(1)} fusion(bf16[9,9,256]{0,1,2:T(8,128)(2,1)} %copy-done.2, bf16[256,1,128]{2,1,0:T(2,128)(2,1)} %copy.126, bf16[256,1,128]{2,1,0:T(2,128)(2,1)S(1)} %copy.125, bf16[256,1,128]{2,1,0:T(2,128)(2,1)S(1)} %copy.124, bf16[256,1,128]{2,1,0:T(2,128)(2,1)} %get-tuple-element.52, ...), kind=kOutput, calls=%fused_computation.17 | convolution fusion | flops 10911744 | bytes 1221120 | tf_op jit(solution)/shard_map/transpose(jvp(ije,ejc->eic))/dot_general | solution.py:40
  206.1 9.3 %scatter_fusion = bf16[64,9,128]{2,1,0:T(8,128)(2,1)S(1)} fusion(bf16[64,9,128]{2,1,0:T(8,128)(2,1)S(1)} %broadcast_in_dim.24, s32[256]{0:T(256)S(1)} %copy-done.9, bf16[256,9,128]{2,1,0:T(8,128)(2,1)S(1)} %fusion.4), kind=kCustom, calls=%fused_computation.1 | custom fusion | flops 294912 | bytes 1770496 | tf_op jit(solution)/shard_map/transpose(jvp(jit(_take)))/scatter-add | solution.py:39
  215.4 1.7 convert_add_fusion
  217.1 2.0 fusion.9
  219.2 39.6 %collective-permute-done.2 = f32[28,96,384]{2,1,0:T(8,128)} collective-permute-done((f32[28,96,384]{2,1,0:T(8,128)}, f32[28,96,384]{2,1,0:T(8,128)}, u32[]{:S(2)}, u32[]{:S(2)}) %collective-permute-start.2) | collective-permute-done | bytes 4128800 | tf_op jit(solution)/shard_map/ppermute | solution.py:12
  258.8 5.9 %add.64 = f32[28,96,384]{2,1,0:T(8,128)} add(f32[28,96,384]{2,1,0:T(8,128)} %add.63, f32[28,96,384]{2,1,0:T(8,128)} %collective-permute-done.2) | non-fusion elementwise | flops 1032192 | bytes 12386304 | tf_op jit(solution)/shard_map/add | solution.py:12
  (53 shorter events, 0.5 us)
Async XLA Ops:
  0.6 169.1 %copy-start = (bf16[28,96,384]{2,1,0:T(8,128)(2,1)S(1)}, bf16[28,96,384]{2,1,0:T(8,128)(2,1)}, u32[]{:S(2)}) copy-start(bf16[28,96,384]{2,1,0:T(8,128)(2,1)} %param.27) | copy-start | bytes 6193156
  0.6 7.0 %copy-start.5 = (bf16[9,9,256]{2,1,0:T(8,128)(2,1)S(1)}, bf16[9,9,256]{2,1,0:T(8,128)(2,1)}, u32[]{:S(2)}) copy-start(bf16[9,9,256]{2,1,0:T(8,128)(2,1)} %param.17) | copy-start | bytes 124420
  2.2 2.2 copy-start.8
  2.9 1.5 copy-start.12
  5.7 3.0 %copy-start.1 = (bf16[64,9,128]{2,0,1:T(8,128)(2,1)S(1)}, bf16[64,9,128]{2,0,1:T(8,128)(2,1)}, u32[]{:S(2)}) copy-start(bf16[64,9,128]{2,0,1:T(8,128)(2,1)} %param.15) | copy-start | bytes 442372
  17.9 3.5 %copy-start.3 = (bf16[256,3,128]{0,2,1:T(8,128)(2,1)}, bf16[256,3,128]{0,2,1:T(8,128)(2,1)S(1)}, u32[]{:S(2)}) copy-start(bf16[256,3,128]{0,2,1:T(8,128)(2,1)S(1)} %copy.98) | copy-start | bytes 589828
  17.9 3.0 %copy-start.14 = (pred[3]{0:T(512)(128)(4,1)S(1)}, pred[3]{0:T(512)(128)(4,1)}, u32[]{:S(2)}) copy-start(pred[3]{0:T(512)(128)(4,1)} %constant.42.clone.1) | copy-start | bytes 13
  20.6 8.8 %copy-start.15 = (s32[64]{0:T(128)S(1)}, s32[64]{0:T(128)}, u32[]{:S(2)}) copy-start(s32[64]{0:T(128)} %param.22) | copy-start | bytes 772
  20.6 8.9 %copy-start.16 = (u32[32]{0:T(128)S(1)}, u32[32]{0:T(128)}, u32[]{:S(2)}) copy-start(u32[32]{0:T(128)} %constant.68) | copy-start | bytes 388
  20.6 10.2 %copy-start.10 = (f32[5,128]{1,0:T(8,128)S(1)}, f32[5,128]{1,0:T(8,128)}, u32[]{:S(2)}) copy-start(f32[5,128]{1,0:T(8,128)} %param.25) | copy-start | bytes 7684
  20.6 10.3 %copy-start.6 = (f32[100,128]{1,0:T(8,128)S(1)}, f32[100,128]{1,0:T(8,128)}, u32[]{:S(2)}) copy-start(f32[100,128]{1,0:T(8,128)} %param.24) | copy-start | bytes 153604
  20.6 10.5 %copy-start.7 = (f32[128,28]{0,1:T(8,128)S(1)}, f32[128,28]{0,1:T(8,128)}, u32[]{:S(2)}) copy-start(f32[128,28]{0,1:T(8,128)} %param.26) | copy-start | bytes 43012
  21.4 23.7 %copy-start.4 = (bf16[256,3,128]{0,2,1:T(8,128)(2,1)}, bf16[256,3,128]{0,2,1:T(8,128)(2,1)S(1)}, u32[]{:S(2)}) copy-start(bf16[256,3,128]{0,2,1:T(8,128)(2,1)S(1)} %copy.112) | copy-start | bytes 589828
  22.5 22.6 %all-to-all-start.1 = ((bf16[4,96,384]{2,1,0:T(8,128)(2,1)}), bf16[4,96,384]{2,1,0:T(8,128)(2,1)S(1)}, u32[]{:S(2)}, u32[]{:S(2)}) async-start(bf16[4,96,384]{2,1,0:T(8,128)(2,1)} %bitcast.24), calls=%async_computation.1 | async-start | bytes 589824 | tf_op jit(solution)/shard_map/all_to_all | solution.py:110
  64.4 7.3 %collective-permute-start = (f32[28,96,384]{2,1,0:T(8,128)}, f32[28,96,384]{2,1,0:T(8,128)S(1)}, u32[]{:S(2)}, u32[]{:S(2)}) collective-permute-start(f32[28,96,384]{2,1,0:T(8,128)} %get-tuple-element.25), channel_id=1, source_target_pairs={{0,1},{1,0},{2,3},{3,2},{4,5},{5,4},{6,7},{7,6},{8,9},{9,8},{10,11... | collective-permute-start | bytes 12386312 | tf_op jit(solution)/shard_map/ppermute | solution.py:12
  74.4 91.3 %collective-permute-start.1 = (f32[28,96,384]{2,1,0:T(8,128)S(1)}, f32[28,96,384]{2,1,0:T(8,128)S(1)}, u32[]{:S(2)}, u32[]{:S(2)}) collective-permute-start(f32[28,96,384]{2,1,0:T(8,128)S(1)} %add.62), channel_id=1, source_target_pairs={{0,2},{1,3},{2,0},{3,1},{4,6},{5,7},{6,4},{7,5},{8,10},{9,11},{10,... | collective-permute-start | bytes 12386312 | tf_op jit(solution)/shard_map/ppermute | solution.py:12
  168.1 90.7 %collective-permute-start.2 = (f32[28,96,384]{2,1,0:T(8,128)}, f32[28,96,384]{2,1,0:T(8,128)}, u32[]{:S(2)}, u32[]{:S(2)}) collective-permute-start(f32[28,96,384]{2,1,0:T(8,128)} %add.63), channel_id=1, source_target_pairs={{0,4},{1,5},{2,6},{3,7},{4,0},{5,1},{6,2},{7,3},{8,12},{9,13},{10,... | collective-permute-start | bytes 12386312 | tf_op jit(solution)/shard_map/ppermute | solution.py:12
  171.9 12.4 %all-to-all-start = ((bf16[4,96,384]{2,1,0:T(8,128)(2,1)}), bf16[4,96,384]{2,1,0:T(8,128)(2,1)S(1)}, u32[]{:S(2)}, u32[]{:S(2)}) async-start(bf16[4,96,384]{2,1,0:T(8,128)(2,1)} %copy.100), calls=%async_computation | async-start | bytes 589824 | tf_op jit(solution)/shard_map/all_to_all | solution.py:99
  177.2 17.1 %copy-start.2 = (bf16[9,9,256]{0,1,2:T(8,128)(2,1)}, bf16[9,9,256]{0,1,2:T(8,128)(2,1)S(1)}, u32[]{:S(2)}) copy-start(bf16[9,9,256]{0,1,2:T(8,128)(2,1)S(1)} %copy.106) | copy-start | bytes 124420
  202.2 3.9 %copy-start.9 = (s32[256]{0:T(256)S(1)}, s32[256]{0:T(256)}, u32[]{:S(2)}) copy-start(s32[256]{0:T(256)} %copy-done.8) | copy-start | bytes 3076
  206.1 11.0 %copy-start.11 = (s32[256]{0:T(256)S(1)}, s32[256]{0:T(256)}, u32[]{:S(2)}) copy-start(s32[256]{0:T(256)} %param.20) | copy-start | bytes 3076
  206.1 11.0 %copy-start.13 = (pred[256]{0:T(512)(128)(4,1)S(1)}, pred[256]{0:T(512)(128)(4,1)}, u32[]{:S(2)}) copy-start(pred[256]{0:T(512)(128)(4,1)} %copy-done.12) | copy-start | bytes 772
